TPU v7x, 32 devices: a whole 2x2x4 slice. The times are simulated.
32 devices in a mesh: gx: 8 (over y, x, core), gy: 4 (over z).
Axes of the slice: x: 2, y: 2, z: 4, core: 2. Of those that a mesh axis runs over, the one named last changes fastest.
Arguments:
- cost: float32 [16, 1024, 512], P(None, 'gx', 'gy'), may hold values from 0 to 7.5
- density_start: float32 [16, 1024, 512], P(None, 'gx', 'gy'), may hold values from 0.125 to 4.5
- coupling: float32 [16, 16], replicated, may hold values from 0 to 0.25
Outputs:
- value: float32 [16, 1024, 512], P(None, 'gx', 'gy')
- density: float32 [16, 1024, 512], P(None, 'gx', 'gy')
- ergodic: float32 [16], replicated
All inputs are finite; a program needn't handle non-finite values.
Results may differ from a plain program's by a relative error of at most 0.0003.
Values sent between devices are 32-bit elements; how exact they have to be, the bound alone decides.
A program may use at most 64 MiB of HBM per device.

v0:
```python
import functools

import jax
import jax.numpy as jnp
from jax import lax
from jax.experimental import pallas as pl
from jax.experimental.pallas import tpu as pltpu
from jax.sharding import PartitionSpec as P

MESH = pl.DeviceIdType.MESH
SWEEPS = 5
THETA = 2.0
PAD = 8
CHUNK = 32
UNROLL = 2


def kernel(
    nx, ny,
    cost_hbm, dens_hbm, coupling,
    trial_hbm, fresh_hbm, means,
    src, u, a, b, d0, d1, cxp, cxm, cyp, cym,
    xs, xr, ps, pr, xs2, xr2, ps2, pr2, edge, edge2, edge3,
    arx_out, arx_in, ary_out, ary_in, lam_tab,
    in_sem, out_sem, hs_sem, hr_sem, axs_sem, axr_sem, ays_sem, ayr_sem,
):
    classes, rows, cols = cost_hbm.shape
    n = nx * ny
    cells = float(n * rows * cols)
    gx, gy = lax.axis_index("gx"), lax.axis_index("gy")
    up, down = lax.rem(gx + nx - 1, nx), lax.rem(gx + 1, nx)
    left, right = lax.rem(gy + ny - 1, ny), lax.rem(gy + 1, ny)

    def at(x, y):
        return {"gx": x, "gy": y}

    peers_x = [at(lax.rem(gx + d, nx), gy) for d in range(1, nx)]
    peers_y = [at(gx, lax.rem(gy + d, ny)) for d in range(1, ny)]

    load_d = pltpu.make_async_copy(dens_hbm, d0.at[:, pl.ds(PAD, rows), :], in_sem.at[0])
    load_c = pltpu.make_async_copy(cost_hbm, src, in_sem.at[1])
    load_d.start()
    load_c.start()

    barrier = pltpu.get_barrier_semaphore()

    for peer in peers_x + peers_y:
        pl.semaphore_signal(barrier, inc=1, device_id=peer, device_id_type=MESH)

    lane = lax.broadcasted_iota(jnp.int32, (1, cols), 1)
    lane_c = lax.broadcasted_iota(jnp.int32, (CHUNK, cols), 1)

    def geometry(w):
        span = 2 * w * classes
        return span, rows // (cols // span)

    def pack(ref, t, k, r0, w):
        span, block = geometry(w)
        p = span * (r0 // block) + 2 * w * k
        q = r0 % block
        turned = pltpu.roll(t, p + w, 1)
        mine = (lane_c >= p) & (lane_c < p + 2 * w)
        ref[q:q + CHUNK, :] = jnp.where(mine, turned, ref[q:q + CHUNK, :])

    def unpack(ref, k, r0, w):
        span, block = geometry(w)
        p = span * (r0 // block) + 2 * w * k
        q = r0 % block
        return pltpu.roll(ref[q:q + CHUNK, :], lax.rem(2 * cols - p, cols), 1)

    def halo_copies(e, w):
        sx, rx, sp, rp = (xs.at[e], xr.at[e], ps.at[e], pr.at[e]) if w == 1 else (xs2, xr2, ps2, pr2)
        plan = (
            (sx.at[0], rx.at[1], at(up, gy)),
            (sx.at[1], rx.at[0], at(down, gy)),
            (sp, rp.at[0], at(gx, right)),
            (sp, rp.at[1], at(gx, left)),
        )
        return [
            pltpu.make_async_remote_copy(
                src_ref=s, dst_ref=r, send_sem=hs_sem.at[e, i], recv_sem=hr_sem.at[e, i],
                device_id=dev, device_id_type=MESH,
            )
            for i, (s, r, dev) in enumerate(plan)
        ]

    def send_halo(e, w):
        copies = halo_copies(e, w)
        for c in copies:
            c.start()
        return copies

    def take_halo(copies, e, w, field):
        for c in copies:
            c.wait_recv()
        rx, rp, ed = (xr.at[e], pr.at[e], edge) if w == 1 else (xr2, pr2, edge2)
        for k in range(classes):
            for j in range(w):
                field[k, PAD - w + j:PAD - w + j + 1, :] = rx[0, j, k:k + 1, :]
                field[k, PAD + rows + j:PAD + rows + j + 1, :] = rx[1, j, k:k + 1, :]
        size = ed.shape[0]
        lanes = lax.broadcasted_iota(jnp.int32, (size, cols), 1)
        ed[...] = jnp.where(
            lax.rem(lanes, 2 * w) < w, rp[0], pltpu.roll(rp[1], cols - 2 * w, 1)
        )

    def edge_rows(ref, field, k, w):
        for j in range(w):
            ref[0, j, pl.ds(k, 1), :] = field[k, PAD + j:PAD + j + 1, :]
            ref[1, j, pl.ds(k, 1), :] = field[k, PAD + rows - w + j:PAD + rows - w + j + 1, :]

    def send_part(s, row, peers, out, into, send_sem, recv_sem):
        out[s] = row
        for i, peer in enumerate(peers):
            pltpu.make_async_remote_copy(
                src_ref=out.at[s], dst_ref=into.at[s, i],
                send_sem=send_sem.at[s], recv_sem=recv_sem.at[s],
                device_id=peer, device_id_type=MESH,
            ).start()

    def send_sums(s, row):
        send_part(s, row, peers_x, arx_out, arx_in, axs_sem, axr_sem)

    def pass_sums(s, row):
        pltpu.make_async_copy(arx_in.at[s], arx_in.at[s], axr_sem.at[s]).wait()
        part = row + jnp.sum(arx_in[s], axis=0)
        send_part(s, part, peers_y, ary_out, ary_in, ays_sem, ayr_sem)
        return part

    def take_sums(s, part):
        pltpu.make_async_copy(ary_in.at[s], ary_in.at[s], ayr_sem.at[s]).wait()
        return part + jnp.sum(ary_in[s], axis=0)

    def fold(x):
        return jnp.sum(x.reshape(CHUNK // 8, 8, cols), axis=0)

    def put(row, place, part):
        return jnp.where(lane == place, jnp.sum(part, axis=(0, 1), keepdims=True), row)

    def spread(row):
        for k in range(classes):
            lam_tab[k] = jnp.broadcast_to(
                jnp.sum(jnp.where(lane == k, row, 0.0), axis=1, keepdims=True), (1, cols)
            )

    def offset_of(total, lam):
        return (total - lam * pltpu.roll(total, cols - classes, 1)) * (1.0 / cells)

    def each_class(body, init):
        return lax.fori_loop(0, classes, body, init, unroll=UNROLL)

    starts = range(0, rows, CHUNK)
    zero_row = jnp.zeros((1, cols), jnp.float32)

    load_d.wait()
    load_c.wait()

    def mix(i, carry):
        r = pl.multiple_of(i * 16, 16)
        parts = [d0[j, pl.ds(PAD + r, 16), :] for j in range(classes)]
        for k in range(classes):
            total = src[k, pl.ds(r, 16), :]
            for j in range(classes):
                total = total + coupling[k, j] * parts[j]
            src[k, pl.ds(r, 16), :] = total
        return carry

    lax.fori_loop(0, rows // 16, mix, 0)

    def first(k, row):
        total = jnp.zeros((8, cols), jnp.float32)
        for r0 in starts:
            t = src[k, r0:r0 + CHUNK, :] * 0.5
            u[k, PAD + r0:PAD + r0 + CHUNK, :] = t
            pack(ps.at[1], t, k, r0, 1)
            pack(ps.at[0], d0[k, PAD + r0:PAD + r0 + CHUNK, :], k, r0, 1)
            total = total + fold(t)
        edge_rows(xs.at[1], u, k, 1)
        edge_rows(xs.at[0], d0, k, 1)
        return put(row, k, total)

    row = each_class(first, zero_row)
    pl.semaphore_wait(barrier, nx + ny - 2)
    copies = send_halo(1, 1)
    send_sums(0, row)
    dens_copies = send_halo(0, 1)
    sent = [copies, dens_copies]
    lam = zero_row
    own = pass_sums(0, row)

    def neighbours(field, ed, k, r0):
        lo = PAD + r0
        mid = field[k, lo:lo + CHUNK, :]
        xp = field[k, lo + 1:lo + 1 + CHUNK, :]
        xm = field[k, lo - 1:lo - 1 + CHUNK, :]
        side = unpack(ed, k, r0, 1)
        yp = jnp.where(lane_c == cols - 1, side, pltpu.roll(mid, cols - 1, 1))
        ym = jnp.where(lane_c == 0, side, pltpu.roll(mid, 1, 1))
        return xp, xm, yp, ym

    def linear(k, row):
        sum_a = jnp.zeros((8, cols), jnp.float32)
        sum_b = jnp.zeros((8, cols), jnp.float32)
        for r0 in starts:
            xp, xm, yp, ym = neighbours(u, edge, k, r0)
            px = jnp.abs(xp - xm) * 0.5
            py = jnp.abs(yp - ym) * 0.5
            sx, sy = xp + xm, yp + ym
            inv = 1.0 / (2.0 + px + py)
            gain = (sx + sy) + px * (sx - px) + py * (sy - py)
            at_a = (src[k, r0:r0 + CHUNK, :] + 0.5 * gain) * inv
            a[k, r0:r0 + CHUNK, :] = at_a
            b[k, r0:r0 + CHUNK, :] = inv
            sum_a = sum_a + fold(at_a)
            sum_b = sum_b + fold(inv)
        return put(put(row, k, sum_a), classes + k, sum_b)

    for s in range(1, SWEEPS):
        take_halo(copies, s, 1, u)
        row = each_class(linear, zero_row)
        send_sums(s, row)
        total = take_sums(s - 1, own)
        offset = offset_of(total, lam)
        lam = THETA * offset
        spread(lam)
        last = s == SWEEPS - 1
        w = 2 if last else 1
        sp, sx = (ps2, xs2) if last else (ps.at[s + 1], xs.at[s + 1])

        def finish(k, carry):
            scale = lam_tab[k]
            for r0 in starts:
                t = a[k, r0:r0 + CHUNK, :] - scale * b[k, r0:r0 + CHUNK, :]
                u[k, PAD + r0:PAD + r0 + CHUNK, :] = t
                pack(sp, t, k, r0, w)
            edge_rows(sx, u, k, w)
            return carry

        each_class(finish, 0)
        copies = send_halo(s + 1, w)
        sent.append(copies)
        own = pass_sums(s, row)

    out_t = pltpu.make_async_copy(u.at[:, pl.ds(PAD, rows), :], trial_hbm, out_sem.at[0])
    out_t.start()
    take_halo(copies, SWEEPS, 2, u)
    take_halo(dens_copies, 0, 1, d0)
    lanes2 = lax.broadcasted_iota(jnp.int32, edge2.shape, 1)
    edge3[...] = jnp.where(
        lax.rem(lanes2, 4) < 2, pltpu.roll(edge2[...], cols - 1, 1), pltpu.roll(edge2[...], 1, 1)
    )

    def flow(field, into, e, c, d, k, r0):
        xp, xm, yp, ym = neighbours(field, edge, k, r0)
        f = c[0] * xp + c[1] * xm + c[2] * yp + c[3] * ym
        into[k, PAD + r0:PAD + r0 + CHUNK, :] = f
        if e is not None:
            pack(ps.at[e], f, k, r0, 1)
            return d
        return d + fold(f)

    base = SWEEPS + 1

    def weigh(k, carry):
        for r0 in starts:
            lo = PAD + r0
            mid = u[k, lo:lo + CHUNK, :]
            xp = u[k, lo + 1:lo + 1 + CHUNK, :]
            xm = u[k, lo - 1:lo - 1 + CHUNK, :]
            xpp = u[k, lo + 2:lo + 2 + CHUNK, :]
            xmm = u[k, lo - 2:lo - 2 + CHUNK, :]
            side = unpack(edge2, k, r0, 2)
            near = unpack(edge3, k, r0, 2)
            ypp = jnp.where(lane_c >= cols - 2, side, pltpu.roll(mid, cols - 2, 1))
            ymm = jnp.where(lane_c < 2, side, pltpu.roll(mid, 2, 1))
            yp = jnp.where(lane_c == cols - 1, near, pltpu.roll(mid, cols - 1, 1))
            ym = jnp.where(lane_c == 0, near, pltpu.roll(mid, 1, 1))
            half = 0.5 / (2.0 + 0.5 * (jnp.abs(xp - xm) + jnp.abs(yp - ym)))
            c = [half * (1.0 + jnp.maximum(far - mid, 0.0)) for far in (xpp, xmm, ypp, ymm)]
            for ref, v in zip((cxp, cxm, cyp, cym), c):
                ref[k, r0:r0 + CHUNK, :] = v
            flow(d0, d1, base, c, None, k, r0)
        edge_rows(xs.at[base], d1, k, 1)
        return carry

    each_class(weigh, 0)
    copies = send_halo(base, 1)
    sent.append(copies)

    field, into = d1, d0
    for s in range(1, SWEEPS):
        take_halo(copies, base + s - 1, 1, field)
        last = s == SWEEPS - 1
        e = None if last else base + s

        def sweep(k, row):
            total = jnp.zeros((8, cols), jnp.float32)
            for r0 in starts:
                c = [ref[k, r0:r0 + CHUNK, :] for ref in (cxp, cxm, cyp, cym)]
                total = flow(field, into, e, c, total, k, r0)
            if last:
                return put(row, k, total)
            edge_rows(xs.at[e], into, k, 1)
            return row

        row = each_class(sweep, zero_row)
        if not last:
            copies = send_halo(e, 1)
            sent.append(copies)
        field, into = into, field

    send_sums(SWEEPS, row)
    out_f = pltpu.make_async_copy(field.at[:, pl.ds(PAD, rows), :], fresh_hbm, out_sem.at[1])
    out_f.start()
    part = pass_sums(SWEEPS, row)
    total = take_sums(SWEEPS - 1, own)
    means[0:1, :] = offset_of(total, lam)
    for copies in sent:
        for c in copies:
            c.wait_send()
    total = take_sums(SWEEPS, part)
    means[1:2, :] = total * (1.0 / cells)
    for s in range(SWEEPS + 1):
        pltpu.make_async_copy(arx_in.at[s], arx_in.at[s], axs_sem.at[s]).wait()
        pltpu.make_async_copy(ary_in.at[s], ary_in.at[s], ays_sem.at[s]).wait()
    out_t.wait()
    out_f.wait()


def shards(cost, density_start, coupling):
    nx, ny = lax.axis_size("gx"), lax.axis_size("gy")
    classes, rows, cols = cost.shape
    f32 = jnp.float32
    full = pltpu.VMEM((classes, rows, cols), f32)
    padded = pltpu.VMEM((classes, rows + 2 * PAD, cols), f32)
    slots = 2 * SWEEPS
    block = rows * 2 * classes // cols
    trial, fresh, means = pl.pallas_call(
        functools.partial(kernel, nx, ny),
        out_shape=(
            jax.ShapeDtypeStruct(cost.shape, f32),
            jax.ShapeDtypeStruct(cost.shape, f32),
            jax.ShapeDtypeStruct((2, cols), f32),
        ),
        in_specs=[
            pl.BlockSpec(memory_space=pl.ANY),
            pl.BlockSpec(memory_space=pl.ANY),
            pl.BlockSpec(memory_space=pltpu.SMEM),
        ],
        out_specs=(
            pl.BlockSpec(memory_space=pl.ANY),
            pl.BlockSpec(memory_space=pl.ANY),
            pl.BlockSpec(memory_space=pltpu.VMEM),
        ),
        scratch_shapes=[
            full, padded, full, full, padded, padded, full, full, full, full,
            pltpu.VMEM((slots, 2, 1, classes, cols), f32),
            pltpu.VMEM((slots, 2, 1, classes, cols), f32),
            pltpu.VMEM((slots, block, cols), f32),
            pltpu.VMEM((slots, 2, block, cols), f32),
            pltpu.VMEM((2, 2, classes, cols), f32),
            pltpu.VMEM((2, 2, classes, cols), f32),
            pltpu.VMEM((2 * block, cols), f32),
            pltpu.VMEM((2, 2 * block, cols), f32),
            pltpu.VMEM((block, cols), f32),
            pltpu.VMEM((2 * block, cols), f32),
            pltpu.VMEM((2 * block, cols), f32),
            pltpu.VMEM((SWEEPS + 1, 1, cols), f32),
            pltpu.VMEM((SWEEPS + 1, nx - 1, 1, cols), f32),
            pltpu.VMEM((SWEEPS + 1, 1, cols), f32),
            pltpu.VMEM((SWEEPS + 1, ny - 1, 1, cols), f32),
            pltpu.VMEM((classes, 1, cols), f32),
            pltpu.SemaphoreType.DMA((2,)),
            pltpu.SemaphoreType.DMA((2,)),
            pltpu.SemaphoreType.DMA((slots, 4)),
            pltpu.SemaphoreType.DMA((slots, 4)),
            pltpu.SemaphoreType.DMA((SWEEPS + 1,)),
            pltpu.SemaphoreType.DMA((SWEEPS + 1,)),
            pltpu.SemaphoreType.DMA((SWEEPS + 1,)),
            pltpu.SemaphoreType.DMA((SWEEPS + 1,)),
        ],
        compiler_params=pltpu.CompilerParams(
            collective_id=0, has_side_effects=True, vmem_limit_bytes=67043328
        ),
    )(cost, density_start, coupling)
    offset = means[0, :classes]
    mass = means[1, :classes]
    value = trial - offset[:, None, None]
    density = fresh / mass[:, None, None]
    return value, density, THETA * offset


def solution(mesh):
    placed = P(None, "gx", "gy")
    return jax.shard_map(
        shards,
        mesh=mesh,
        in_specs=(placed, placed, P()),
        out_specs=(placed, placed, P()),
        check_vma=False,
    )
```

profile of v0, /device:TPU:0, one launch (start us, length us, event | category | flops | bytes accessed | tf_op | source)
XLA Modules:
  0.0 84.9 jit_solution(4185459949378424375)
XLA Ops:
  0.6 80.1 %shard_map.58 = (f32[16,128,128]{2,1,0:T(8,128)}, f32[16,128,128]{2,1,0:T(8,128)}, f32[2,128]{1,0:T(2,128)}) custom-call(f32[16,128,128]{2,1,0:T(8,128)} %cost_hbm.1, f32[16,128,128]{2,1,0:T(8,128)} %dens_hbm.1, f32[16,16]{1,0:T(8,128)} %coupling.1), custom_call_target="tpu_custom_call" | custom-call | tf_op jit(solution)/shard_map/pallas_call | solution.py:338
  80.7 0.0 copy-start
  80.8 0.6 copy-done
  81.4 0.5 broadcast_multiply_fusion
  81.9 3.0 %broadcast_divide_fusion = (f32[16,128,128]{2,1,0:T(8,128)}, f32[16,128,128]{2,1,0:T(8,128)}) fusion(f32[16,128,128]{2,1,0:T(8,128)} %get-tuple-element.8, f32[16]{0:T(128)S(1)} %get-tuple-element.9, f32[16,128,128]{2,1,0:T(8,128)} %get-tuple-element.6, f32[16]{0:T(128)S(1)} %get-tuple-element.10), kind=kLoop, calls=%fused_computation | loop fusion | flops 524288 | bytes 4194432 | tf_op jit(solution)/shard_map/div | solution.py:389
  (1 shorter events, 0.0 us)
Async XLA Ops:
  80.7 0.7 copy-start
where the time goes:
time: 85.2 us; the launch traced here: 84.9 us
  Pallas kernels  80.1 us (94%)
  other arithmetic  3.53 us (4%)
    pallas_call x1, Pallas kernels, shards(): pl.pallas_call(functools.partial(kernel, nx, ny), out_shape=(jax.ShapeDty...  80.1 us
    div x1, other arithmetic, shards(): density = fresh / mass[:, None, None]  3.02 us

commit v1 on v0

v1 whole, which is shorter than its diff:
```python
import functools

import jax
import jax.numpy as jnp
from jax import lax
from jax.experimental import pallas as pl
from jax.experimental.pallas import tpu as pltpu
from jax.sharding import PartitionSpec as P

MESH = pl.DeviceIdType.MESH
SWEEPS = 5
THETA = 2.0
PAD = 8
CHUNK = 32
SUB = 8
GROUP = 4


def kernel(
    nx, ny,
    cost_hbm, dens_hbm, coupling,
    trial, fresh, means,
    src, u, a, b, d, cxp, cxm, cyp, cym,
    xs, xr, ps, pr, xs2, xr2, ps2, pr2,
    ar_out, ar_in, lam_tab,
    in_sem, hs_sem, hr_sem, as_sem, ar_sem,
):
    classes, rows, cols = cost_hbm.shape
    groups = classes // GROUP
    n = nx * ny
    cells = float(n * rows * cols)
    gx, gy = lax.axis_index("gx"), lax.axis_index("gy")
    up, down = lax.rem(gx + nx - 1, nx), lax.rem(gx + 1, nx)
    left, right = lax.rem(gy + ny - 1, ny), lax.rem(gy + 1, ny)
    me = gx * ny + gy

    def at(x, y):
        return {"gx": x, "gy": y}

    def each_peer(body):
        def step(i, carry):
            dx, dy = i // ny, lax.rem(i, ny)
            body(at(lax.rem(gx + dx, nx), lax.rem(gy + dy, ny)))
            return carry

        lax.fori_loop(1, n, step, 0, unroll=n - 1 if n <= 32 else 1)

    load_d = pltpu.make_async_copy(dens_hbm, d.at[0, :, pl.ds(PAD, rows), :], in_sem.at[0])
    load_c = pltpu.make_async_copy(cost_hbm, src, in_sem.at[1])
    load_d.start()
    load_c.start()

    barrier = pltpu.get_barrier_semaphore()
    each_peer(lambda dev: pl.semaphore_signal(barrier, inc=1, device_id=dev, device_id_type=MESH))

    lane = lax.broadcasted_iota(jnp.int32, (SUB, cols), 1)
    sub = lax.broadcasted_iota(jnp.int32, (SUB, cols), 0)
    lane_c = lax.broadcasted_iota(jnp.int32, (CHUNK, cols), 1)
    pair = {w: lane // (2 * w) for w in (1, 2)}

    def geometry(w):
        span = 2 * w * GROUP
        return span, rows // (cols // span)

    def pack(accs, t, k, r0, w):
        span, block = geometry(w)
        accs = list(accs)
        for i in range(CHUNK // SUB):
            r = r0 + SUB * i
            p = span * (r // block) + 2 * w * k
            q = (r % block) // SUB
            turned = pltpu.roll(t[SUB * i:SUB * i + SUB], (p + w) % cols, 1)
            accs[q] = jnp.where(pair[w] == p // (2 * w), turned, accs[q])
        return accs

    def unpack(ed, k, r0, w):
        span, block = geometry(w)
        parts = []
        for i in range(CHUNK // SUB):
            r = r0 + SUB * i
            p = span * (r // block) + 2 * w * k
            q = r % block
            parts.append(pltpu.roll(ed[q:q + SUB], (cols - p) % cols, 1))
        return jnp.concatenate(parts, axis=0)

    def empty(w):
        return [jnp.zeros((SUB, cols), jnp.float32) for _ in range(geometry(w)[1] // SUB)]

    def halo_copies(e, g, w):
        i = e * groups + g
        sx, rx, sp, rp = (
            (xs.at[i], xr.at[i], ps.at[i], pr.at[i]) if w == 1
            else (xs2.at[g], xr2.at[g], ps2.at[g], pr2.at[g])
        )
        plan = (
            (sp, rp.at[0], at(gx, right)),
            (sp, rp.at[1], at(gx, left)),
            (sx.at[0], rx.at[1], at(up, gy)),
            (sx.at[1], rx.at[0], at(down, gy)),
        )
        return [
            pltpu.make_async_remote_copy(
                src_ref=s, dst_ref=r, send_sem=hs_sem.at[i, j], recv_sem=hr_sem.at[i, j],
                device_id=dev, device_id_type=MESH,
            )
            for j, (s, r, dev) in enumerate(plan)
        ]

    def send_halo(e, g, w, accs):
        i = e * groups + g
        ref = ps.at[i] if w == 1 else ps2.at[g]
        for q, v in enumerate(accs):
            ref[SUB * q:SUB * q + SUB, :] = v
        for c in halo_copies(e, g, w):
            c.start()

    def take_halo(e, g, w, field):
        i = e * groups + g
        for c in halo_copies(e, g, w):
            c.wait_recv()
        rx, rp = (xr.at[i], pr.at[i]) if w == 1 else (xr2.at[g], pr2.at[g])
        for k in range(GROUP):
            for j in range(w):
                m = j * GROUP + k
                field[g * GROUP + k, PAD - w + j:PAD - w + j + 1, :] = rx[0, m:m + 1, :]
                field[g * GROUP + k, PAD + rows + j:PAD + rows + j + 1, :] = rx[1, m:m + 1, :]
        size = geometry(w)[1]
        lanes = lax.broadcasted_iota(jnp.int32, (size, cols), 1)
        return jnp.where(
            lax.rem(lanes, 2 * w) < w, rp[0], pltpu.roll(rp[1], cols - 2 * w, 1)
        )

    def edge_rows(e, g, k, w, first, last):
        i = e * groups + g
        ref = xs.at[i] if w == 1 else xs2.at[g]
        for j in range(w):
            m = j * GROUP + k
            ref[0, m:m + 1, :] = first[j:j + 1]
            ref[1, m:m + 1, :] = last[CHUNK - w + j:CHUNK - w + j + 1]

    def fold(x):
        return jnp.sum(x.reshape(CHUNK // SUB, SUB, cols), axis=0)

    def put(acc, place, part):
        return jnp.where(sub == place, jnp.sum(part, axis=0, keepdims=True), acc)

    def send_sums(s, g, acc):
        i = s * groups + g
        line = jnp.sum(acc, axis=1, keepdims=True)
        row = jnp.sum(jnp.where(lane == sub, line, 0.0), axis=0, keepdims=True)
        ar_out[i] = row
        ar_in[i, me] = row

        def send(dev):
            pltpu.make_async_remote_copy(
                src_ref=ar_out.at[i], dst_ref=ar_in.at[i, me],
                send_sem=as_sem.at[i], recv_sem=ar_sem.at[i],
                device_id=dev, device_id_type=MESH,
            ).start()

        each_peer(send)

    def take_sums(s, g):
        i = s * groups + g
        got = ar_in.at[i, pl.ds(0, n - 1)]
        pltpu.make_async_copy(got, got, ar_sem.at[i]).wait()
        total = jnp.sum(ar_in[i], axis=0)
        line = jnp.sum(jnp.where(lane == sub, total, 0.0), axis=1, keepdims=True)
        return jnp.broadcast_to(line, (SUB, cols))

    def offset_of(g, total):
        return (total - lam_tab[g] * pltpu.roll(total, GROUP, 0)) * (1.0 / cells)

    starts = range(0, rows, CHUNK)
    zero8 = jnp.zeros((SUB, cols), jnp.float32)

    load_d.wait()
    load_c.wait()

    def begin(g, carry):
        def mix(r8, carry):
            r = pl.multiple_of(r8 * SUB, SUB)
            totals = [src[g * GROUP + k, pl.ds(r, SUB), :] for k in range(GROUP)]
            for j in range(classes):
                part = d[0, j, pl.ds(PAD + r, SUB), :]
                for k in range(GROUP):
                    totals[k] = totals[k] + coupling[g * GROUP + k, j] * part
            for k in range(GROUP):
                src[g * GROUP + k, pl.ds(r, SUB), :] = totals[k]
            return carry

        lax.fori_loop(0, rows // SUB, mix, 0, unroll=2)
        acc, accs, accs_d = zero8, empty(1), empty(1)
        for k in range(GROUP):
            kk = g * GROUP + k
            total = zero8
            ts, ds = [], []
            for r0 in starts:
                t = src[kk, r0:r0 + CHUNK, :] * 0.5
                dd = d[0, kk, PAD + r0:PAD + r0 + CHUNK, :]
                u[kk, PAD + r0:PAD + r0 + CHUNK, :] = t
                accs = pack(accs, t, k, r0, 1)
                accs_d = pack(accs_d, dd, k, r0, 1)
                total = total + fold(t)
                ts.append(t)
                ds.append(dd)
            edge_rows(1, g, k, 1, ts[0], ts[-1])
            edge_rows(0, g, k, 1, ds[0], ds[-1])
            acc = put(acc, k, total)
        lam_tab[g] = zero8

        @pl.when(g == 0)
        def _():
            pl.semaphore_wait(barrier, n - 1)

        send_halo(1, g, 1, accs)
        send_sums(0, g, acc)
        send_halo(0, g, 1, accs_d)
        return carry

    lax.fori_loop(0, groups, begin, 0)

    def neighbours(field, ed, kk, k, r0):
        lo = PAD + r0
        mid = field[kk, lo:lo + CHUNK, :]
        xp = field[kk, lo + 1:lo + 1 + CHUNK, :]
        xm = field[kk, lo - 1:lo - 1 + CHUNK, :]
        side = unpack(ed, k, r0, 1)
        yp = jnp.where(lane_c == cols - 1, side, pltpu.roll(mid, cols - 1, 1))
        ym = jnp.where(lane_c == 0, side, pltpu.roll(mid, 1, 1))
        return xp, xm, yp, ym

    def climb(s, g, w):
        ed = take_halo(s, g, 1, u)
        acc = zero8
        for k in range(GROUP):
            kk = g * GROUP + k
            sum_a, sum_b = zero8, zero8
            for r0 in starts:
                xp, xm, yp, ym = neighbours(u, ed, kk, k, r0)
                px = jnp.abs(xp - xm) * 0.5
                py = jnp.abs(yp - ym) * 0.5
                sx, sy = xp + xm, yp + ym
                inv = 1.0 / (2.0 + px + py)
                gain = (sx + sy) + px * (sx - px) + py * (sy - py)
                at_a = (src[kk, r0:r0 + CHUNK, :] + 0.5 * gain) * inv
                a[kk, r0:r0 + CHUNK, :] = at_a
                b[kk, r0:r0 + CHUNK, :] = inv
                sum_a = sum_a + fold(at_a)
                sum_b = sum_b + fold(inv)
            acc = put(put(acc, k, sum_a), GROUP + k, sum_b)
        send_sums(s, g, acc)
        lam_tab[g] = THETA * offset_of(g, take_sums(s - 1, g))
        accs = empty(w)
        for k in range(GROUP):
            kk = g * GROUP + k
            scale = lam_tab[g, k:k + 1, :]
            ts = []
            for r0 in starts:
                t = a[kk, r0:r0 + CHUNK, :] - scale * b[kk, r0:r0 + CHUNK, :]
                u[kk, PAD + r0:PAD + r0 + CHUNK, :] = t
                if w == 2:
                    trial[kk, r0:r0 + CHUNK, :] = t
                accs = pack(accs, t, k, r0, w)
                ts.append(t)
            edge_rows(s + 1, g, k, w, ts[0], ts[-1])
        send_halo(s + 1, g, w, accs)

    def middle(i, carry):
        climb(1 + i // groups, lax.rem(i, groups), 1)
        return carry

    def final(g, carry):
        climb(SWEEPS - 1, g, 2)
        return carry

    lax.fori_loop(0, (SWEEPS - 2) * groups, middle, 0)
    lax.fori_loop(0, groups, final, 0)

    base = SWEEPS + 1

    def weigh(g, carry):
        ed2 = take_halo(SWEEPS, g, 2, u)
        ed = take_halo(0, g, 1, d.at[0])
        lanes2 = lax.broadcasted_iota(jnp.int32, ed2.shape, 1)
        ed3 = jnp.where(
            lax.rem(lanes2, 4) < 2, pltpu.roll(ed2, cols - 1, 1), pltpu.roll(ed2, 1, 1)
        )
        accs = empty(1)
        for k in range(GROUP):
            kk = g * GROUP + k
            fs = []
            for r0 in starts:
                lo = PAD + r0
                mid = u[kk, lo:lo + CHUNK, :]
                xp = u[kk, lo + 1:lo + 1 + CHUNK, :]
                xm = u[kk, lo - 1:lo - 1 + CHUNK, :]
                xpp = u[kk, lo + 2:lo + 2 + CHUNK, :]
                xmm = u[kk, lo - 2:lo - 2 + CHUNK, :]
                side = unpack(ed2, k, r0, 2)
                near = unpack(ed3, k, r0, 2)
                ypp = jnp.where(lane_c >= cols - 2, side, pltpu.roll(mid, cols - 2, 1))
                ymm = jnp.where(lane_c < 2, side, pltpu.roll(mid, 2, 1))
                yp = jnp.where(lane_c == cols - 1, near, pltpu.roll(mid, cols - 1, 1))
                ym = jnp.where(lane_c == 0, near, pltpu.roll(mid, 1, 1))
                half = 0.5 / (2.0 + 0.5 * (jnp.abs(xp - xm) + jnp.abs(yp - ym)))
                c = [half * (1.0 + jnp.maximum(far - mid, 0.0)) for far in (xpp, xmm, ypp, ymm)]
                for ref, v in zip((cxp, cxm, cyp, cym), c):
                    ref[kk, r0:r0 + CHUNK, :] = v
                xp, xm, yp, ym = neighbours(d.at[0], ed, kk, k, r0)
                f = c[0] * xp + c[1] * xm + c[2] * yp + c[3] * ym
                d[1, kk, lo:lo + CHUNK, :] = f
                accs = pack(accs, f, k, r0, 1)
                fs.append(f)
            edge_rows(base, g, k, 1, fs[0], fs[-1])
        send_halo(base, g, 1, accs)
        return carry

    lax.fori_loop(0, groups, weigh, 0)

    def flow(s, g, last):
        now, then = lax.rem(s, 2), lax.rem(s + 1, 2)
        ed = take_halo(base + s - 1, g, 1, d.at[now])
        accs, acc = empty(1), zero8
        for k in range(GROUP):
            kk = g * GROUP + k
            fs, total = [], zero8
            for r0 in starts:
                c = [ref[kk, r0:r0 + CHUNK, :] for ref in (cxp, cxm, cyp, cym)]
                xp, xm, yp, ym = neighbours(d.at[now], ed, kk, k, r0)
                f = c[0] * xp + c[1] * xm + c[2] * yp + c[3] * ym
                if last:
                    fresh[kk, r0:r0 + CHUNK, :] = f
                    total = total + fold(f)
                else:
                    d[then, kk, PAD + r0:PAD + r0 + CHUNK, :] = f
                    accs = pack(accs, f, k, r0, 1)
                    fs.append(f)
            if last:
                acc = put(acc, k, total)
            else:
                edge_rows(base + s, g, k, 1, fs[0], fs[-1])
        if last:
            send_sums(SWEEPS, g, acc)
        else:
            send_halo(base + s, g, 1, accs)

    def flows(i, carry):
        flow(1 + i // groups, lax.rem(i, groups), False)
        return carry

    def last_flow(g, carry):
        flow(SWEEPS - 1, g, True)
        return carry

    lax.fori_loop(0, (SWEEPS - 2) * groups, flows, 0)
    lax.fori_loop(0, groups, last_flow, 0)

    def flat(g, line, row):
        mine = (lane == g * GROUP + sub) & (sub < GROUP)
        return row + jnp.sum(jnp.where(mine, line, 0.0), axis=0, keepdims=True)

    def shifts(g, row):
        return flat(g, offset_of(g, take_sums(SWEEPS - 1, g)), row)

    def drain(i, carry):
        for c in halo_copies(i // groups, lax.rem(i, groups), 1):
            c.wait_send()
        return carry

    def drain2(g, carry):
        for c in halo_copies(SWEEPS, g, 2):
            c.wait_send()
        return carry

    def drain_sums(i, carry):
        got = ar_in.at[i, pl.ds(0, n - 1)]
        pltpu.make_async_copy(got, got, as_sem.at[i]).wait()
        return carry

    zero_row = jnp.zeros((1, cols), jnp.float32)
    means[0:1, :] = lax.fori_loop(0, groups, shifts, zero_row)
    lax.fori_loop(0, SWEEPS * groups, drain, 0)
    lax.fori_loop(0, groups, drain2, 0)
    lax.fori_loop((SWEEPS + 1) * groups, 2 * SWEEPS * groups, drain, 0)
    lax.fori_loop(0, (SWEEPS + 1) * groups, drain_sums, 0)

    def masses(g, row):
        return flat(g, take_sums(SWEEPS, g) * (1.0 / cells), row)

    means[1:2, :] = lax.fori_loop(0, groups, masses, zero_row)


def shards(cost, density_start, coupling):
    nx, ny = lax.axis_size("gx"), lax.axis_size("gy")
    classes, rows, cols = cost.shape
    f32 = jnp.float32
    n = nx * ny
    groups = classes // GROUP
    full = pltpu.VMEM((classes, rows, cols), f32)
    slots = 2 * SWEEPS * groups
    sums = (SWEEPS + 1) * groups
    block = rows * 2 * GROUP // cols
    trial, fresh, means = pl.pallas_call(
        functools.partial(kernel, nx, ny),
        out_shape=(
            jax.ShapeDtypeStruct(cost.shape, f32),
            jax.ShapeDtypeStruct(cost.shape, f32),
            jax.ShapeDtypeStruct((2, cols), f32),
        ),
        in_specs=[
            pl.BlockSpec(memory_space=pl.ANY),
            pl.BlockSpec(memory_space=pl.ANY),
            pl.BlockSpec(memory_space=pltpu.SMEM),
        ],
        out_specs=(
            pl.BlockSpec(memory_space=pltpu.VMEM),
            pl.BlockSpec(memory_space=pltpu.VMEM),
            pl.BlockSpec(memory_space=pltpu.VMEM),
        ),
        scratch_shapes=[
            full, pltpu.VMEM((classes, rows + 2 * PAD, cols), f32), full, full,
            pltpu.VMEM((2, classes, rows + 2 * PAD, cols), f32), full, full, full, full,
            pltpu.VMEM((slots, 2, GROUP, cols), f32),
            pltpu.VMEM((slots, 2, GROUP, cols), f32),
            pltpu.VMEM((slots, block, cols), f32),
            pltpu.VMEM((slots, 2, block, cols), f32),
            pltpu.VMEM((groups, 2, 2 * GROUP, cols), f32),
            pltpu.VMEM((groups, 2, 2 * GROUP, cols), f32),
            pltpu.VMEM((groups, 2 * block, cols), f32),
            pltpu.VMEM((groups, 2, 2 * block, cols), f32),
            pltpu.VMEM((sums, 1, cols), f32),
            pltpu.VMEM((sums, n, 1, cols), f32),
            pltpu.VMEM((groups, SUB, cols), f32),
            pltpu.SemaphoreType.DMA((2,)),
            pltpu.SemaphoreType.DMA((slots, 4)),
            pltpu.SemaphoreType.DMA((slots, 4)),
            pltpu.SemaphoreType.DMA((sums,)),
            pltpu.SemaphoreType.DMA((sums,)),
        ],
        compiler_params=pltpu.CompilerParams(
            collective_id=0, has_side_effects=True, vmem_limit_bytes=VMEM_LIMIT
        ),
    )(cost, density_start, coupling)
    offset = means[0, :classes]
    mass = means[1, :classes]
    value = trial - offset[:, None, None]
    density = fresh / mass[:, None, None]
    return value, density, THETA * offset


VMEM_LIMIT = 67043328


def solution(mesh):
    placed = P(None, "gx", "gy")
    return jax.shard_map(
        shards,
        mesh=mesh,
        in_specs=(placed, placed, P()),
        out_specs=(placed, placed, P()),
        check_vma=False,
    )
```

time: 85.2 us -> 70.6 us (0.83)
  Pallas kernels: 80.1 us -> 65.5 us
    pallas_call x1, Pallas kernels: 80.1 us -> 65.5 us  [shards(): pl.pallas_call(functools.partial(kernel, nx, ny), out_shape=(jax.ShapeDty...]
where the time goes in v1:
time: 70.6 us; the launch traced here: 70.3 us
  Pallas kernels  65.5 us (93%)
  other arithmetic  3.53 us (5%)
    pallas_call x1, Pallas kernels, shards(): pl.pallas_call(functools.partial(kernel, nx, ny), out_shape=(jax.ShapeDty...  65.5 us
    div x1, other arithmetic, shards(): density = fresh / mass[:, None, None]  3.02 us

profile of v1, /device:TPU:0, one launch (start us, length us, event | category | flops | bytes accessed | tf_op | source)
XLA Modules:
  0.0 70.3 jit_solution(15916372657015311825)
XLA Ops:
  0.6 65.5 %shard_map.58 = (f32[16,128,128]{2,1,0:T(8,128)}, f32[16,128,128]{2,1,0:T(8,128)}, f32[2,128]{1,0:T(2,128)}) custom-call(f32[16,128,128]{2,1,0:T(8,128)} %cost_hbm.1, f32[16,128,128]{2,1,0:T(8,128)} %dens_hbm.1, f32[16,16]{1,0:T(8,128)} %coupling.1), custom_call_target="tpu_custom_call" | custom-call | tf_op jit(solution)/shard_map/pallas_call | solution.py:404
  66.1 0.0 copy-start
  66.1 0.6 copy-done
  66.8 0.5 broadcast_multiply_fusion
  67.3 3.0 %broadcast_divide_fusion = (f32[16,128,128]{2,1,0:T(8,128)}, f32[16,128,128]{2,1,0:T(8,128)}) fusion(f32[16,128,128]{2,1,0:T(8,128)} %get-tuple-element.8, f32[16]{0:T(128)S(1)} %get-tuple-element.9, f32[16,128,128]{2,1,0:T(8,128)} %get-tuple-element.6, f32[16]{0:T(128)S(1)} %get-tuple-element.10), kind=kLoop, calls=%fused_computation | loop fusion | flops 524288 | bytes 4194432 | tf_op jit(solution)/shard_map/div | solution.py:448
  (1 shorter events, 0.0 us)
Async XLA Ops:
  66.1 0.7 copy-start

commit v2 on v1

--- a/solution.py
+++ b/solution.py
@@ -18,9 +18,9 @@
 
 def kernel(
     nx, ny,
-    cost_hbm, dens_hbm, coupling,
+    cost_hbm, dens_hbm, coup_hbm,
     trial, fresh, means,
-    src, u, a, b, d, cxp, cxm, cyp, cym,
+    coupling, src, u, a, b, d0, d1, cxp, cxm, cyp, cym,
     xs, xr, ps, pr, xs2, xr2, ps2, pr2,
     ar_out, ar_in, lam_tab,
     in_sem, hs_sem, hr_sem, as_sem, ar_sem,
@@ -45,10 +45,12 @@
 
         lax.fori_loop(1, n, step, 0, unroll=n - 1 if n <= 32 else 1)
 
-    load_d = pltpu.make_async_copy(dens_hbm, d.at[0, :, pl.ds(PAD, rows), :], in_sem.at[0])
+    load_d = pltpu.make_async_copy(dens_hbm, d0.at[:, pl.ds(PAD, rows), :], in_sem.at[0])
     load_c = pltpu.make_async_copy(cost_hbm, src, in_sem.at[1])
+    load_k = pltpu.make_async_copy(coup_hbm, coupling, in_sem.at[2])
     load_d.start()
     load_c.start()
+    load_k.start()
 
     barrier = pltpu.get_barrier_semaphore()
     each_peer(lambda dev: pl.semaphore_signal(barrier, inc=1, device_id=dev, device_id_type=MESH))
@@ -176,13 +178,14 @@
 
     load_d.wait()
     load_c.wait()
+    load_k.wait()
 
     def begin(g, carry):
         def mix(r8, carry):
             r = pl.multiple_of(r8 * SUB, SUB)
             totals = [src[g * GROUP + k, pl.ds(r, SUB), :] for k in range(GROUP)]
             for j in range(classes):
-                part = d[0, j, pl.ds(PAD + r, SUB), :]
+                part = d0[j, pl.ds(PAD + r, SUB), :]
                 for k in range(GROUP):
                     totals[k] = totals[k] + coupling[g * GROUP + k, j] * part
             for k in range(GROUP):
@@ -197,7 +200,7 @@
             ts, ds = [], []
             for r0 in starts:
                 t = src[kk, r0:r0 + CHUNK, :] * 0.5
-                dd = d[0, kk, PAD + r0:PAD + r0 + CHUNK, :]
+                dd = d0[kk, PAD + r0:PAD + r0 + CHUNK, :]
                 u[kk, PAD + r0:PAD + r0 + CHUNK, :] = t
                 accs = pack(accs, t, k, r0, 1)
                 accs_d = pack(accs_d, dd, k, r0, 1)
@@ -281,7 +284,7 @@
 
     def weigh(g, carry):
         ed2 = take_halo(SWEEPS, g, 2, u)
-        ed = take_halo(0, g, 1, d.at[0])
+        ed = take_halo(0, g, 1, d0)
         lanes2 = lax.broadcasted_iota(jnp.int32, ed2.shape, 1)
         ed3 = jnp.where(
             lax.rem(lanes2, 4) < 2, pltpu.roll(ed2, cols - 1, 1), pltpu.roll(ed2, 1, 1)
@@ -307,9 +310,9 @@
                 c = [half * (1.0 + jnp.maximum(far - mid, 0.0)) for far in (xpp, xmm, ypp, ymm)]
                 for ref, v in zip((cxp, cxm, cyp, cym), c):
                     ref[kk, r0:r0 + CHUNK, :] = v
-                xp, xm, yp, ym = neighbours(d.at[0], ed, kk, k, r0)
+                xp, xm, yp, ym = neighbours(d0, ed, kk, k, r0)
                 f = c[0] * xp + c[1] * xm + c[2] * yp + c[3] * ym
-                d[1, kk, lo:lo + CHUNK, :] = f
+                d1[kk, lo:lo + CHUNK, :] = f
                 accs = pack(accs, f, k, r0, 1)
                 fs.append(f)
             edge_rows(base, g, k, 1, fs[0], fs[-1])
@@ -319,21 +322,21 @@
     lax.fori_loop(0, groups, weigh, 0)
 
     def flow(s, g, last):
-        now, then = lax.rem(s, 2), lax.rem(s + 1, 2)
-        ed = take_halo(base + s - 1, g, 1, d.at[now])
+        now, then = (d1, d0) if s % 2 else (d0, d1)
+        ed = take_halo(base + s - 1, g, 1, now)
         accs, acc = empty(1), zero8
         for k in range(GROUP):
             kk = g * GROUP + k
             fs, total = [], zero8
             for r0 in starts:
                 c = [ref[kk, r0:r0 + CHUNK, :] for ref in (cxp, cxm, cyp, cym)]
-                xp, xm, yp, ym = neighbours(d.at[now], ed, kk, k, r0)
+                xp, xm, yp, ym = neighbours(now, ed, kk, k, r0)
                 f = c[0] * xp + c[1] * xm + c[2] * yp + c[3] * ym
                 if last:
                     fresh[kk, r0:r0 + CHUNK, :] = f
                     total = total + fold(f)
                 else:
-                    d[then, kk, PAD + r0:PAD + r0 + CHUNK, :] = f
+                    then[kk, PAD + r0:PAD + r0 + CHUNK, :] = f
                     accs = pack(accs, f, k, r0, 1)
                     fs.append(f)
             if last:
@@ -345,16 +348,13 @@
         else:
             send_halo(base + s, g, 1, accs)
 
-    def flows(i, carry):
-        flow(1 + i // groups, lax.rem(i, groups), False)
-        return carry
-
-    def last_flow(g, carry):
-        flow(SWEEPS - 1, g, True)
-        return carry
-
-    lax.fori_loop(0, (SWEEPS - 2) * groups, flows, 0)
-    lax.fori_loop(0, groups, last_flow, 0)
+    for s in range(1, SWEEPS):
+
+        def flows(g, carry):
+            flow(s, g, s == SWEEPS - 1)
+            return carry
+
+        lax.fori_loop(0, groups, flows, 0)
 
     def flat(g, line, row):
         mine = (lane == g * GROUP + sub) & (sub < GROUP)
@@ -398,6 +398,7 @@
     n = nx * ny
     groups = classes // GROUP
     full = pltpu.VMEM((classes, rows, cols), f32)
+    padded = pltpu.VMEM((classes, rows + 2 * PAD, cols), f32)
     slots = 2 * SWEEPS * groups
     sums = (SWEEPS + 1) * groups
     block = rows * 2 * GROUP // cols
@@ -411,7 +412,7 @@
         in_specs=[
             pl.BlockSpec(memory_space=pl.ANY),
             pl.BlockSpec(memory_space=pl.ANY),
-            pl.BlockSpec(memory_space=pltpu.SMEM),
+            pl.BlockSpec(memory_space=pl.ANY),
         ],
         out_specs=(
             pl.BlockSpec(memory_space=pltpu.VMEM),
@@ -419,8 +420,9 @@
             pl.BlockSpec(memory_space=pltpu.VMEM),
         ),
         scratch_shapes=[
-            full, pltpu.VMEM((classes, rows + 2 * PAD, cols), f32), full, full,
-            pltpu.VMEM((2, classes, rows + 2 * PAD, cols), f32), full, full, full, full,
+            pltpu.SMEM(coupling.shape, f32),
+            full, padded, full, full,
+            padded, padded, full, full, full, full,
             pltpu.VMEM((slots, 2, GROUP, cols), f32),
             pltpu.VMEM((slots, 2, GROUP, cols), f32),
             pltpu.VMEM((slots, block, cols), f32),
@@ -432,7 +434,7 @@
             pltpu.VMEM((sums, 1, cols), f32),
             pltpu.VMEM((sums, n, 1, cols), f32),
             pltpu.VMEM((groups, SUB, cols), f32),
-            pltpu.SemaphoreType.DMA((2,)),
+            pltpu.SemaphoreType.DMA((3,)),
             pltpu.SemaphoreType.DMA((slots, 4)),
             pltpu.SemaphoreType.DMA((slots, 4)),
             pltpu.SemaphoreType.DMA((sums,)),
@@ -449,7 +451,7 @@
     return value, density, THETA * offset
 
 
-VMEM_LIMIT = 67043328
+VMEM_LIMIT = 54000000
 
 
 def solution(mesh):

time: 70.6 us -> 62.3 us (0.88)
  Pallas kernels: 65.5 us -> 58.8 us
  other arithmetic: 3.53 us -> 1.99 us
    pallas_call x1, Pallas kernels: 65.5 us -> 58.8 us  [shards(): pl.pallas_call(functools.partial(kernel, nx, ny), out_shape=(jax.ShapeDty...]
    div x1, other arithmetic: 3.02 us -> 1.48 us  [shards(): density = fresh / mass[:, None, None]]
where the time goes in v2:
time: 62.3 us; the launch traced here: 62.1 us
  Pallas kernels  58.8 us (94%)
  other arithmetic  1.99 us (3%)
  local copies, waits for them, and re-layouts  0.69 us (1%)
  between operations  0.65 us (1%)
    pallas_call x1, Pallas kernels, shards(): pl.pallas_call(functools.partial(kernel, nx, ny), out_shape=(jax.ShapeDty...  58.8 us
    div x1, other arithmetic, shards(): density = fresh / mass[:, None, None]  1.48 us

profile of v2, /device:TPU:0, one launch (start us, length us, event | category | flops | bytes accessed | tf_op | source)
XLA Modules:
  0.0 62.1 jit_solution(1954844249063406271)
XLA Ops:
  0.6 0.0 copy-start
  0.6 0.7 %copy-done = f32[16,16]{1,0:T(8,128)S(1)} copy-done((f32[16,16]{1,0:T(8,128)S(1)}, f32[16,16]{1,0:T(8,128)}, u32[]{:S(2)}) %copy-start) | copy-done | bytes 1048
  1.3 58.8 %shard_map.58 = (f32[16,128,128]{2,1,0:T(8,128)S(1)}, f32[16,128,128]{2,1,0:T(8,128)S(1)}, f32[2,128]{1,0:T(2,128)S(1)}) custom-call(f32[16,128,128]{2,1,0:T(8,128)} %cost_hbm.1, f32[16,128,128]{2,1,0:T(8,128)} %dens_hbm.1, f32[16,16]{1,0:T(8,128)S(1)} %copy-done), custom_call_target="tpu_custom_call" | custom-call | tf_op jit(solution)/shard_map/pallas_call | solution.py:405
  60.1 0.5 broadcast_multiply_fusion
  60.6 1.5 %broadcast_divide_fusion = (f32[16,128,128]{2,1,0:T(8,128)}, f32[16,128,128]{2,1,0:T(8,128)}) fusion(f32[16,128,128]{2,1,0:T(8,128)S(1)} %get-tuple-element.8, f32[16]{0:T(128)S(1)} %get-tuple-element.9, f32[16,128,128]{2,1,0:T(8,128)S(1)} %get-tuple-element.6, f32[16]{0:T(128)S(1)} %get-tuple-element.10), kind=kLoop, calls=%fused_computation | loop fusion | flops 524288 | bytes 4194432 | tf_op jit(solution)/shard_map/div | solution.py:450
  (1 shorter events, 0.0 us)
Async XLA Ops:
  0.6 0.7 %copy-start = (f32[16,16]{1,0:T(8,128)S(1)}, f32[16,16]{1,0:T(8,128)}, u32[]{:S(2)}) copy-start(f32[16,16]{1,0:T(8,128)} %coup_hbm.1) | copy-start | bytes 3076

commit v3 on v2

--- a/solution.py
+++ b/solution.py
@@ -116,7 +116,7 @@
         for c in halo_copies(e, g, w):
             c.start()
 
-    def take_halo(e, g, w, field):
+    def take_halo(e, g, w, above, below):
         i = e * groups + g
         for c in halo_copies(e, g, w):
             c.wait_recv()
@@ -124,8 +124,8 @@
         for k in range(GROUP):
             for j in range(w):
                 m = j * GROUP + k
-                field[g * GROUP + k, PAD - w + j:PAD - w + j + 1, :] = rx[0, m:m + 1, :]
-                field[g * GROUP + k, PAD + rows + j:PAD + rows + j + 1, :] = rx[1, m:m + 1, :]
+                above[g * GROUP + k, PAD - w + j:PAD - w + j + 1, :] = rx[0, m:m + 1, :]
+                below[g * GROUP + k, PAD + rows + j:PAD + rows + j + 1, :] = rx[1, m:m + 1, :]
         size = geometry(w)[1]
         lanes = lax.broadcasted_iota(jnp.int32, (size, cols), 1)
         return jnp.where(
@@ -234,7 +234,7 @@
         return xp, xm, yp, ym
 
     def climb(s, g, w):
-        ed = take_halo(s, g, 1, u)
+        ed = take_halo(s, g, 1, u, u)
         acc = zero8
         for k in range(GROUP):
             kk = g * GROUP + k
@@ -281,18 +281,17 @@
     lax.fori_loop(0, groups, final, 0)
 
     base = SWEEPS + 1
-
-    def weigh(g, carry):
-        ed2 = take_halo(SWEEPS, g, 2, u)
-        ed = take_halo(0, g, 1, d0)
+    extra = 2 * SWEEPS
+
+    def weights(g):
+        ed2 = take_halo(SWEEPS, g, 2, u, u)
         lanes2 = lax.broadcasted_iota(jnp.int32, ed2.shape, 1)
         ed3 = jnp.where(
             lax.rem(lanes2, 4) < 2, pltpu.roll(ed2, cols - 1, 1), pltpu.roll(ed2, 1, 1)
         )
-        accs = empty(1)
-        for k in range(GROUP):
-            kk = g * GROUP + k
-            fs = []
+        for k in range(GROUP):
+            kk = g * GROUP + k
+            cs = []
             for r0 in starts:
                 lo = PAD + r0
                 mid = u[kk, lo:lo + CHUNK, :]
@@ -308,53 +307,68 @@
                 ym = jnp.where(lane_c == 0, near, pltpu.roll(mid, 1, 1))
                 half = 0.5 / (2.0 + 0.5 * (jnp.abs(xp - xm) + jnp.abs(yp - ym)))
                 c = [half * (1.0 + jnp.maximum(far - mid, 0.0)) for far in (xpp, xmm, ypp, ymm)]
-                for ref, v in zip((cxp, cxm, cyp, cym), c):
-                    ref[kk, r0:r0 + CHUNK, :] = v
-                xp, xm, yp, ym = neighbours(d0, ed, kk, k, r0)
-                f = c[0] * xp + c[1] * xm + c[2] * yp + c[3] * ym
-                d1[kk, lo:lo + CHUNK, :] = f
-                accs = pack(accs, f, k, r0, 1)
-                fs.append(f)
-            edge_rows(base, g, k, 1, fs[0], fs[-1])
-        send_halo(base, g, 1, accs)
-        return carry
-
-    lax.fori_loop(0, groups, weigh, 0)
-
-    def flow(s, g, last):
+                cxp[kk, lo:lo + CHUNK, :] = c[0]
+                cxm[kk, lo:lo + CHUNK, :] = c[1]
+                cyp[kk, r0:r0 + CHUNK, :] = c[2]
+                cym[kk, r0:r0 + CHUNK, :] = c[3]
+                cs.append(c)
+            edge_rows(extra, g, k, 1, cs[0][1], cs[-1][0])
+
+    def send_weights(g):
+        accs = empty(1)
+        for k in range(GROUP):
+            kk = g * GROUP + k
+            for r0 in starts:
+                rim = jnp.where(lane_c == 0, cym[kk, r0:r0 + CHUNK, :], cyp[kk, r0:r0 + CHUNK, :])
+                accs = pack(accs, rim, k, r0, 1)
+        send_halo(extra, g, 1, accs)
+
+    def flow(s, g):
+        last, counted = s == SWEEPS - 1, s == SWEEPS - 2
         now, then = (d1, d0) if s % 2 else (d0, d1)
-        ed = take_halo(base + s - 1, g, 1, now)
+        ed = take_halo(base + s - 1 if s else 0, g, 1, now, now)
         accs, acc = empty(1), zero8
         for k in range(GROUP):
             kk = g * GROUP + k
             fs, total = [], zero8
             for r0 in starts:
-                c = [ref[kk, r0:r0 + CHUNK, :] for ref in (cxp, cxm, cyp, cym)]
+                lo = PAD + r0
+                c = [
+                    cxp[kk, lo:lo + CHUNK, :], cxm[kk, lo:lo + CHUNK, :],
+                    cyp[kk, r0:r0 + CHUNK, :], cym[kk, r0:r0 + CHUNK, :],
+                ]
                 xp, xm, yp, ym = neighbours(now, ed, kk, k, r0)
                 f = c[0] * xp + c[1] * xm + c[2] * yp + c[3] * ym
                 if last:
                     fresh[kk, r0:r0 + CHUNK, :] = f
-                    total = total + fold(f)
-                else:
-                    then[kk, PAD + r0:PAD + r0 + CHUNK, :] = f
-                    accs = pack(accs, f, k, r0, 1)
-                    fs.append(f)
-            if last:
+                    continue
+                then[kk, lo:lo + CHUNK, :] = f
+                accs = pack(accs, f, k, r0, 1)
+                fs.append(f)
+                if counted:
+                    total = total + fold(f * a[kk, r0:r0 + CHUNK, :])
+            if not last:
+                edge_rows(base + s, g, k, 1, fs[0], fs[-1])
+            if counted:
                 acc = put(acc, k, total)
-            else:
-                edge_rows(base + s, g, k, 1, fs[0], fs[-1])
-        if last:
+        if not last:
+            send_halo(base + s, g, 1, accs)
+        if counted:
             send_sums(SWEEPS, g, acc)
-        else:
-            send_halo(base + s, g, 1, accs)
-
-    for s in range(1, SWEEPS):
-
-        def flows(g, carry):
-            flow(s, g, s == SWEEPS - 1)
-            return carry
-
-        lax.fori_loop(0, groups, flows, 0)
+
+    def shares(g):
+        ed = take_halo(extra, g, 1, cxp, cxm)
+        for k in range(GROUP):
+            kk = g * GROUP + k
+            for r0 in starts:
+                lo = PAD + r0
+                side = unpack(ed, k, r0, 1)
+                east = pltpu.roll(cym[kk, r0:r0 + CHUNK, :], cols - 1, 1)
+                west = pltpu.roll(cyp[kk, r0:r0 + CHUNK, :], 1, 1)
+                a[kk, r0:r0 + CHUNK, :] = (
+                    (cxp[kk, lo - 1:lo - 1 + CHUNK, :] + cxm[kk, lo + 1:lo + 1 + CHUNK, :])
+                    + (jnp.where(lane_c == cols - 1, side, east) + jnp.where(lane_c == 0, side, west))
+                )
 
     def flat(g, line, row):
         mine = (lane == g * GROUP + sub) & (sub < GROUP)
@@ -378,17 +392,38 @@
         pltpu.make_async_copy(got, got, as_sem.at[i]).wait()
         return carry
 
-    zero_row = jnp.zeros((1, cols), jnp.float32)
-    means[0:1, :] = lax.fori_loop(0, groups, shifts, zero_row)
-    lax.fori_loop(0, SWEEPS * groups, drain, 0)
-    lax.fori_loop(0, groups, drain2, 0)
-    lax.fori_loop((SWEEPS + 1) * groups, 2 * SWEEPS * groups, drain, 0)
-    lax.fori_loop(0, (SWEEPS + 1) * groups, drain_sums, 0)
-
-    def masses(g, row):
-        return flat(g, take_sums(SWEEPS, g) * (1.0 / cells), row)
-
-    means[1:2, :] = lax.fori_loop(0, groups, masses, zero_row)
+    end = base + SWEEPS - 2
+    for s in range(SWEEPS):
+
+        def flows(g, carry):
+            if s == 0:
+                weights(g)
+            flow(s, g)
+            if s == 0:
+                send_weights(g)
+            if s == SWEEPS - 3:
+                shares(g)
+            return carry
+
+        if s == SWEEPS - 1:
+            means[0:1, :] = lax.fori_loop(0, groups, shifts, jnp.zeros((1, cols), jnp.float32))
+            lax.fori_loop(0, SWEEPS * groups, drain, 0)
+            lax.fori_loop(0, groups, drain2, 0)
+            lax.fori_loop(base * groups, end * groups, drain, 0)
+            lax.fori_loop(extra * groups, (extra + 1) * groups, drain, 0)
+            lax.fori_loop(0, SWEEPS * groups, drain_sums, 0)
+        lax.fori_loop(0, groups, flows, 0)
+
+    lax.fori_loop(end * groups, (end + 1) * groups, drain, 0)
+    row = jnp.zeros((1, cols), jnp.float32)
+    for g in range(groups):
+        i = SWEEPS * groups + g
+        drain_sums(i, 0)
+        got = ar_in.at[i, pl.ds(0, n - 1)]
+        pltpu.make_async_copy(got, got, ar_sem.at[i]).wait()
+        total = jnp.where(lane[0:1] < GROUP, jnp.sum(ar_in[i], axis=0), 0.0)
+        row = row + (total if g == 0 else pltpu.roll(total, g * GROUP, 1))
+    means[1:2, :] = row * (1.0 / cells)
 
 
 def shards(cost, density_start, coupling):
@@ -399,7 +434,7 @@
     groups = classes // GROUP
     full = pltpu.VMEM((classes, rows, cols), f32)
     padded = pltpu.VMEM((classes, rows + 2 * PAD, cols), f32)
-    slots = 2 * SWEEPS * groups
+    slots = (2 * SWEEPS + 1) * groups
     sums = (SWEEPS + 1) * groups
     block = rows * 2 * GROUP // cols
     trial, fresh, means = pl.pallas_call(
@@ -422,7 +457,7 @@
         scratch_shapes=[
             pltpu.SMEM(coupling.shape, f32),
             full, padded, full, full,
-            padded, padded, full, full, full, full,
+            padded, padded, padded, padded, full, full,
             pltpu.VMEM((slots, 2, GROUP, cols), f32),
             pltpu.VMEM((slots, 2, GROUP, cols), f32),
             pltpu.VMEM((slots, block, cols), f32),

time: 62.3 us -> 56.3 us (0.904)
  Pallas kernels: 58.8 us -> 52.8 us
    pallas_call x1, Pallas kernels: 58.8 us -> 52.8 us  [shards(): pl.pallas_call(functools.partial(kernel, nx, ny), out_shape=(jax.ShapeDty...]
where the time goes in v3:
time: 56.3 us; the launch traced here: 56.1 us
  Pallas kernels  52.8 us (94%)
  other arithmetic  1.99 us (4%)
  local copies, waits for them, and re-layouts  0.69 us (1%)
  between operations  0.65 us (1%)
    pallas_call x1, Pallas kernels, shards(): pl.pallas_call(functools.partial(kernel, nx, ny), out_shape=(jax.ShapeDty...  52.8 us
    div x1, other arithmetic, shards(): density = fresh / mass[:, None, None]  1.48 us

profile of v3, /device:TPU:0, one launch (start us, length us, event | category | flops | bytes accessed | tf_op | source)
XLA Modules:
  0.0 56.1 jit_solution(10380866198446770151)
XLA Ops:
  0.6 0.0 copy-start
  0.6 0.7 %copy-done = f32[16,16]{1,0:T(8,128)S(1)} copy-done((f32[16,16]{1,0:T(8,128)S(1)}, f32[16,16]{1,0:T(8,128)}, u32[]{:S(2)}) %copy-start) | copy-done | bytes 1048
  1.3 52.8 %shard_map.58 = (f32[16,128,128]{2,1,0:T(8,128)S(1)}, f32[16,128,128]{2,1,0:T(8,128)S(1)}, f32[2,128]{1,0:T(2,128)S(1)}) custom-call(f32[16,128,128]{2,1,0:T(8,128)} %cost_hbm.1, f32[16,128,128]{2,1,0:T(8,128)} %dens_hbm.1, f32[16,16]{1,0:T(8,128)S(1)} %copy-done), custom_call_target="tpu_custom_call" | custom-call | tf_op jit(solution)/shard_map/pallas_call | solution.py:440
  54.1 0.5 broadcast_multiply_fusion
  54.6 1.5 %broadcast_divide_fusion = (f32[16,128,128]{2,1,0:T(8,128)}, f32[16,128,128]{2,1,0:T(8,128)}) fusion(f32[16,128,128]{2,1,0:T(8,128)S(1)} %get-tuple-element.8, f32[16]{0:T(128)S(1)} %get-tuple-element.9, f32[16,128,128]{2,1,0:T(8,128)S(1)} %get-tuple-element.6, f32[16]{0:T(128)S(1)} %get-tuple-element.10), kind=kLoop, calls=%fused_computation | loop fusion | flops 524288 | bytes 4194432 | tf_op jit(solution)/shard_map/div | solution.py:485
  (1 shorter events, 0.0 us)
Async XLA Ops:
  0.6 0.7 %copy-start = (f32[16,16]{1,0:T(8,128)S(1)}, f32[16,16]{1,0:T(8,128)}, u32[]{:S(2)}) copy-start(f32[16,16]{1,0:T(8,128)} %coup_hbm.1) | copy-start | bytes 3076

commit v4 on v3

--- a/solution.py
+++ b/solution.py
@@ -102,7 +102,7 @@
         )
         return [
             pltpu.make_async_remote_copy(
-                src_ref=s, dst_ref=r, send_sem=hs_sem.at[i, j], recv_sem=hr_sem.at[i, j],
+                src_ref=s, dst_ref=r, send_sem=hs_sem.at[e, j // 2], recv_sem=hr_sem.at[i, j // 2],
                 device_id=dev, device_id_type=MESH,
             )
             for j, (s, r, dev) in enumerate(plan)
@@ -116,11 +116,14 @@
         for c in halo_copies(e, g, w):
             c.start()
 
+    def settle(ref, sem):
+        pltpu.make_async_copy(ref, ref, sem).wait()
+
     def take_halo(e, g, w, above, below):
         i = e * groups + g
-        for c in halo_copies(e, g, w):
-            c.wait_recv()
         rx, rp = (xr.at[i], pr.at[i]) if w == 1 else (xr2.at[g], pr2.at[g])
+        settle(rp, hr_sem.at[i, 0])
+        settle(rx, hr_sem.at[i, 1])
         for k in range(GROUP):
             for j in range(w):
                 m = j * GROUP + k
@@ -156,7 +159,7 @@
         def send(dev):
             pltpu.make_async_remote_copy(
                 src_ref=ar_out.at[i], dst_ref=ar_in.at[i, me],
-                send_sem=as_sem.at[i], recv_sem=ar_sem.at[i],
+                send_sem=as_sem.at[s], recv_sem=ar_sem.at[i],
                 device_id=dev, device_id_type=MESH,
             ).start()
 
@@ -164,8 +167,7 @@
 
     def take_sums(s, g):
         i = s * groups + g
-        got = ar_in.at[i, pl.ds(0, n - 1)]
-        pltpu.make_async_copy(got, got, ar_sem.at[i]).wait()
+        settle(ar_in.at[i, pl.ds(0, n - 1)], ar_sem.at[i])
         total = jnp.sum(ar_in[i], axis=0)
         line = jnp.sum(jnp.where(lane == sub, total, 0.0), axis=1, keepdims=True)
         return jnp.broadcast_to(line, (SUB, cols))
@@ -377,20 +379,14 @@
     def shifts(g, row):
         return flat(g, offset_of(g, take_sums(SWEEPS - 1, g)), row)
 
-    def drain(i, carry):
-        for c in halo_copies(i // groups, lax.rem(i, groups), 1):
-            c.wait_send()
-        return carry
-
-    def drain2(g, carry):
-        for c in halo_copies(SWEEPS, g, 2):
-            c.wait_send()
-        return carry
-
-    def drain_sums(i, carry):
-        got = ar_in.at[i, pl.ds(0, n - 1)]
-        pltpu.make_async_copy(got, got, as_sem.at[i]).wait()
-        return carry
+    def drain(e):
+        part = pl.ds(e * groups, groups)
+        rx, rp = (xr2, pr2) if e == SWEEPS else (xr.at[part], pr.at[part])
+        settle(rp, hs_sem.at[e, 0])
+        settle(rx, hs_sem.at[e, 1])
+
+    def drain_sums(s):
+        settle(ar_in.at[pl.ds(s * groups, groups), pl.ds(0, n - 1)], as_sem.at[s])
 
     end = base + SWEEPS - 2
     for s in range(SWEEPS):
@@ -407,20 +403,18 @@
 
         if s == SWEEPS - 1:
             means[0:1, :] = lax.fori_loop(0, groups, shifts, jnp.zeros((1, cols), jnp.float32))
-            lax.fori_loop(0, SWEEPS * groups, drain, 0)
-            lax.fori_loop(0, groups, drain2, 0)
-            lax.fori_loop(base * groups, end * groups, drain, 0)
-            lax.fori_loop(extra * groups, (extra + 1) * groups, drain, 0)
-            lax.fori_loop(0, SWEEPS * groups, drain_sums, 0)
+            for e in [*range(end), extra]:
+                drain(e)
+            for j in range(SWEEPS):
+                drain_sums(j)
         lax.fori_loop(0, groups, flows, 0)
 
-    lax.fori_loop(end * groups, (end + 1) * groups, drain, 0)
+    drain(end)
+    drain_sums(SWEEPS)
     row = jnp.zeros((1, cols), jnp.float32)
     for g in range(groups):
         i = SWEEPS * groups + g
-        drain_sums(i, 0)
-        got = ar_in.at[i, pl.ds(0, n - 1)]
-        pltpu.make_async_copy(got, got, ar_sem.at[i]).wait()
+        settle(ar_in.at[i, pl.ds(0, n - 1)], ar_sem.at[i])
         total = jnp.where(lane[0:1] < GROUP, jnp.sum(ar_in[i], axis=0), 0.0)
         row = row + (total if g == 0 else pltpu.roll(total, g * GROUP, 1))
     means[1:2, :] = row * (1.0 / cells)
@@ -470,9 +464,9 @@
             pltpu.VMEM((sums, n, 1, cols), f32),
             pltpu.VMEM((groups, SUB, cols), f32),
             pltpu.SemaphoreType.DMA((3,)),
-            pltpu.SemaphoreType.DMA((slots, 4)),
-            pltpu.SemaphoreType.DMA((slots, 4)),
-            pltpu.SemaphoreType.DMA((sums,)),
+            pltpu.SemaphoreType.DMA((2 * SWEEPS + 1, 2)),
+            pltpu.SemaphoreType.DMA((slots, 2)),
+            pltpu.SemaphoreType.DMA((SWEEPS + 1,)),
             pltpu.SemaphoreType.DMA((sums,)),
         ],
         compiler_params=pltpu.CompilerParams(

time: 56.3 us -> 54 us (0.959)
  Pallas kernels: 52.8 us -> 50.4 us
    pallas_call x1, Pallas kernels: 52.8 us -> 50.4 us  [shards(): pl.pallas_call(functools.partial(kernel, nx, ny), out_shape=(jax.ShapeDty...]
where the time goes in v4:
time: 54 us; the launch traced here: 53.8 us
  Pallas kernels  50.4 us (93%)
  other arithmetic  1.99 us (4%)
  local copies, waits for them, and re-layouts  0.69 us (1%)
  between operations  0.65 us (1%)
    pallas_call x1, Pallas kernels, shards(): pl.pallas_call(functools.partial(kernel, nx, ny), out_shape=(jax.ShapeDty...  50.4 us
    div x1, other arithmetic, shards(): density = fresh / mass[:, None, None]  1.48 us

profile of v4, /device:TPU:0, one launch (start us, length us, event | category | flops | bytes accessed | tf_op | source)
XLA Modules:
  0.0 53.8 jit_solution(9905340143366875937)
XLA Ops:
  0.6 0.0 copy-start
  0.6 0.7 %copy-done = f32[16,16]{1,0:T(8,128)S(1)} copy-done((f32[16,16]{1,0:T(8,128)S(1)}, f32[16,16]{1,0:T(8,128)}, u32[]{:S(2)}) %copy-start) | copy-done | bytes 1048
  1.3 50.4 %shard_map.58 = (f32[16,128,128]{2,1,0:T(8,128)S(1)}, f32[16,128,128]{2,1,0:T(8,128)S(1)}, f32[2,128]{1,0:T(2,128)S(1)}) custom-call(f32[16,128,128]{2,1,0:T(8,128)} %cost_hbm.1, f32[16,128,128]{2,1,0:T(8,128)} %dens_hbm.1, f32[16,16]{1,0:T(8,128)S(1)} %copy-done), custom_call_target="tpu_custom_call" | custom-call | tf_op jit(solution)/shard_map/pallas_call | solution.py:434
  51.8 0.5 broadcast_multiply_fusion
  52.3 1.5 %broadcast_divide_fusion = (f32[16,128,128]{2,1,0:T(8,128)}, f32[16,128,128]{2,1,0:T(8,128)}) fusion(f32[16,128,128]{2,1,0:T(8,128)S(1)} %get-tuple-element.8, f32[16]{0:T(128)S(1)} %get-tuple-element.9, f32[16,128,128]{2,1,0:T(8,128)S(1)} %get-tuple-element.6, f32[16]{0:T(128)S(1)} %get-tuple-element.10), kind=kLoop, calls=%fused_computation | loop fusion | flops 524288 | bytes 4194432 | tf_op jit(solution)/shard_map/div | solution.py:479
  (1 shorter events, 0.0 us)
Async XLA Ops:
  0.6 0.7 %copy-start = (f32[16,16]{1,0:T(8,128)S(1)}, f32[16,16]{1,0:T(8,128)}, u32[]{:S(2)}) copy-start(f32[16,16]{1,0:T(8,128)} %coup_hbm.1) | copy-start | bytes 3076

commit v5 on v4

--- a/solution.py
+++ b/solution.py
@@ -183,18 +183,18 @@
     load_k.wait()
 
     def begin(g, carry):
-        def mix(r8, carry):
-            r = pl.multiple_of(r8 * SUB, SUB)
-            totals = [src[g * GROUP + k, pl.ds(r, SUB), :] for k in range(GROUP)]
+        def mix(i, carry):
+            r = pl.multiple_of(i * CHUNK, CHUNK)
+            totals = [src[g * GROUP + k, pl.ds(r, CHUNK), :] for k in range(GROUP)]
             for j in range(classes):
-                part = d0[j, pl.ds(PAD + r, SUB), :]
+                part = d0[j, pl.ds(PAD + r, CHUNK), :]
                 for k in range(GROUP):
                     totals[k] = totals[k] + coupling[g * GROUP + k, j] * part
             for k in range(GROUP):
-                src[g * GROUP + k, pl.ds(r, SUB), :] = totals[k]
+                src[g * GROUP + k, pl.ds(r, CHUNK), :] = totals[k]
             return carry
 
-        lax.fori_loop(0, rows // SUB, mix, 0, unroll=2)
+        lax.fori_loop(0, rows // CHUNK, mix, 0)
         acc, accs, accs_d = zero8, empty(1), empty(1)
         for k in range(GROUP):
             kk = g * GROUP + k
@@ -395,7 +395,7 @@
             if s == 0:
                 weights(g)
             flow(s, g)
-            if s == 0:
+            if s == 1:
                 send_weights(g)
             if s == SWEEPS - 3:
                 shares(g)

time: 54 us -> 53.3 us (0.987)
  Pallas kernels: 50.4 us -> 49.7 us
    pallas_call x1, Pallas kernels: 50.4 us -> 49.7 us  [shards(): pl.pallas_call(functools.partial(kernel, nx, ny), out_shape=(jax.ShapeDty...]
where the time goes in v5:
time: 53.3 us; the launch traced here: 53 us
  Pallas kernels  49.7 us (93%)
  other arithmetic  1.99 us (4%)
  local copies, waits for them, and re-layouts  0.69 us (1%)
  between operations  0.65 us (1%)
    pallas_call x1, Pallas kernels, shards(): pl.pallas_call(functools.partial(kernel, nx, ny), out_shape=(jax.ShapeDty...  49.7 us
    div x1, other arithmetic, shards(): density = fresh / mass[:, None, None]  1.48 us

profile of v5, /device:TPU:0, one launch (start us, length us, event | category | flops | bytes accessed | tf_op | source)
XLA Modules:
  0.0 53.0 jit_solution(7817927631345298567)
XLA Ops:
  0.6 0.0 copy-start
  0.6 0.7 %copy-done = f32[16,16]{1,0:T(8,128)S(1)} copy-done((f32[16,16]{1,0:T(8,128)S(1)}, f32[16,16]{1,0:T(8,128)}, u32[]{:S(2)}) %copy-start) | copy-done | bytes 1048
  1.3 49.7 %shard_map.58 = (f32[16,128,128]{2,1,0:T(8,128)S(1)}, f32[16,128,128]{2,1,0:T(8,128)S(1)}, f32[2,128]{1,0:T(2,128)S(1)}) custom-call(f32[16,128,128]{2,1,0:T(8,128)} %cost_hbm.1, f32[16,128,128]{2,1,0:T(8,128)} %dens_hbm.1, f32[16,16]{1,0:T(8,128)S(1)} %copy-done), custom_call_target="tpu_custom_call" | custom-call | tf_op jit(solution)/shard_map/pallas_call | solution.py:434
  51.0 0.5 broadcast_multiply_fusion
  51.6 1.5 %broadcast_divide_fusion = (f32[16,128,128]{2,1,0:T(8,128)}, f32[16,128,128]{2,1,0:T(8,128)}) fusion(f32[16,128,128]{2,1,0:T(8,128)S(1)} %get-tuple-element.8, f32[16]{0:T(128)S(1)} %get-tuple-element.9, f32[16,128,128]{2,1,0:T(8,128)S(1)} %get-tuple-element.6, f32[16]{0:T(128)S(1)} %get-tuple-element.10), kind=kLoop, calls=%fused_computation | loop fusion | flops 524288 | bytes 4194432 | tf_op jit(solution)/shard_map/div | solution.py:479
  (1 shorter events, 0.0 us)
Async XLA Ops:
  0.6 0.7 %copy-start = (f32[16,16]{1,0:T(8,128)S(1)}, f32[16,16]{1,0:T(8,128)}, u32[]{:S(2)}) copy-start(f32[16,16]{1,0:T(8,128)} %coup_hbm.1) | copy-start | bytes 3076

commit v6 on v5

--- a/solution.py
+++ b/solution.py
@@ -43,7 +43,11 @@
             body(at(lax.rem(gx + dx, nx), lax.rem(gy + dy, ny)))
             return carry
 
-        lax.fori_loop(1, n, step, 0, unroll=n - 1 if n <= 32 else 1)
+        if n > 32:
+            lax.fori_loop(1, n, step, 0)
+            return
+        for i in sorted(range(1, n), key=lambda i: -min(i // ny, nx - i // ny)):
+            step(i, 0)
 
     load_d = pltpu.make_async_copy(dens_hbm, d0.at[:, pl.ds(PAD, rows), :], in_sem.at[0])
     load_c = pltpu.make_async_copy(cost_hbm, src, in_sem.at[1])
@@ -218,8 +222,8 @@
         def _():
             pl.semaphore_wait(barrier, n - 1)
 
+        send_sums(0, g, acc)
         send_halo(1, g, 1, accs)
-        send_sums(0, g, acc)
         send_halo(0, g, 1, accs_d)
         return carry
 

time: 53.3 us -> 53.2 us (level)
  no operation moved by 1% of the time
where the time goes in v6:
time: 53.2 us; the launch traced here: 52.9 us
  Pallas kernels  49.6 us (93%)
  other arithmetic  1.99 us (4%)
  local copies, waits for them, and re-layouts  0.69 us (1%)
  between operations  0.65 us (1%)
    pallas_call x1, Pallas kernels, shards(): pl.pallas_call(functools.partial(kernel, nx, ny), out_shape=(jax.ShapeDty...  49.6 us
    div x1, other arithmetic, shards(): density = fresh / mass[:, None, None]  1.48 us

profile of v6, /device:TPU:0, one launch (start us, length us, event | category | flops | bytes accessed | tf_op | source)
XLA Modules:
  0.0 52.9 jit_solution(11485653496668372608)
XLA Ops:
  0.6 0.0 copy-start
  0.6 0.7 %copy-done = f32[16,16]{1,0:T(8,128)S(1)} copy-done((f32[16,16]{1,0:T(8,128)S(1)}, f32[16,16]{1,0:T(8,128)}, u32[]{:S(2)}) %copy-start) | copy-done | bytes 1048
  1.3 49.6 %shard_map.58 = (f32[16,128,128]{2,1,0:T(8,128)S(1)}, f32[16,128,128]{2,1,0:T(8,128)S(1)}, f32[2,128]{1,0:T(2,128)S(1)}) custom-call(f32[16,128,128]{2,1,0:T(8,128)} %cost_hbm.1, f32[16,128,128]{2,1,0:T(8,128)} %dens_hbm.1, f32[16,16]{1,0:T(8,128)S(1)} %copy-done), custom_call_target="tpu_custom_call" | custom-call | tf_op jit(solution)/shard_map/pallas_call | solution.py:438
  50.9 0.5 broadcast_multiply_fusion
  51.5 1.5 %broadcast_divide_fusion = (f32[16,128,128]{2,1,0:T(8,128)}, f32[16,128,128]{2,1,0:T(8,128)}) fusion(f32[16,128,128]{2,1,0:T(8,128)S(1)} %get-tuple-element.8, f32[16]{0:T(128)S(1)} %get-tuple-element.9, f32[16,128,128]{2,1,0:T(8,128)S(1)} %get-tuple-element.6, f32[16]{0:T(128)S(1)} %get-tuple-element.10), kind=kLoop, calls=%fused_computation | loop fusion | flops 524288 | bytes 4194432 | tf_op jit(solution)/shard_map/div | solution.py:483
  (1 shorter events, 0.0 us)
Async XLA Ops:
  0.6 0.7 %copy-start = (f32[16,16]{1,0:T(8,128)S(1)}, f32[16,16]{1,0:T(8,128)}, u32[]{:S(2)}) copy-start(f32[16,16]{1,0:T(8,128)} %coup_hbm.1) | copy-start | bytes 3076
